TPU v7x, 64 devices: a 2x2x8 block of a 4x4x8 slice. The times are simulated.
64 devices in a mesh: dp: 4 (over x, y), tp: 16 (over z, core).
Axes of the slice: x: 2, y: 2, z: 8, core: 2. Of those that a mesh axis runs over, the one named last changes fastest.
The devices are a block of a 4x4x8 slice.
Arguments:
- x: bfloat16 [4, 256, 4096], P('dp', 'tp'), parts along dimension 0
- ln_gain: bfloat16 [2, 4096], replicated
- ln_bias: bfloat16 [2, 4096], replicated
- w_q: bfloat16 [2, 4096, 16, 256], P(None, None, 'tp')
- b_q: bfloat16 [2, 16, 256], P(None, 'tp')
- w_k: bfloat16 [2, 4096, 16, 256], P(None, None, 'tp')
- b_k: bfloat16 [2, 16, 256], P(None, 'tp')
- w_v: bfloat16 [2, 4096, 16, 256], P(None, None, 'tp')
- b_v: bfloat16 [2, 16, 256], P(None, 'tp')
- w_o: bfloat16 [2, 16, 256, 4096], P(None, 'tp')
- b_o: bfloat16 [2, 4096], replicated
- w_up: bfloat16 [2, 4096, 16384], P(None, None, 'tp')
- b_up: bfloat16 [2, 16384], P(None, 'tp')
- w_down: bfloat16 [2, 16384, 4096], P(None, 'tp')
- b_down: bfloat16 [2, 4096], replicated
Outputs:
- output: bfloat16 [4, 256, 4096], P('dp', 'tp'), parts along dimension 0
There are 4 independent parts. A program takes and returns all parts, laid end to end along the dimension named above; an argument that names none is the same for every part.
All inputs are finite; a program needn't handle non-finite values.
Results may differ from a plain program's by a relative error of at most 0.02.
Values are sent between devices in bfloat16 or wider.
A program may use at most 768 MiB of HBM per device.

v0:
```python
import jax
import jax.numpy as jnp
from jax import lax
from jax.sharding import PartitionSpec as P

ROT_DIM = 32
ROPE_BASE = 10000.0
LN_EPS = 1e-5


def rotary_tables(seq_len):
    half = ROT_DIM // 2
    inv_freq = 1.0 / (ROPE_BASE ** (jnp.arange(half, dtype=jnp.float32) * (2.0 / ROT_DIM)))
    angles = jnp.arange(seq_len, dtype=jnp.float32)[:, None] * inv_freq[None, :]
    return jnp.cos(angles), jnp.sin(angles)


def apply_rotary(projected, cosine, sine):
    half = ROT_DIM // 2
    first = projected[..., :half]
    second = projected[..., half:ROT_DIM]
    return jnp.concatenate([first * cosine - second * sine, second * cosine + first * sine, projected[..., ROT_DIM:]], axis=-1)


def layer_norm(hidden, gain, bias):
    x_f32 = hidden.astype(jnp.float32)
    mean = jnp.mean(x_f32, axis=-1, keepdims=True)
    centered = x_f32 - mean
    variance = jnp.mean(centered * centered, axis=-1, keepdims=True)
    return (centered * lax.rsqrt(variance + LN_EPS) * gain.astype(jnp.float32) + bias.astype(jnp.float32)).astype(jnp.bfloat16)


def causal_attention(q_rot, k_rot, values):
    seq_len = q_rot.shape[2]
    head_dim = q_rot.shape[3]
    scores = jnp.einsum("bhqe,bhke->bhqk", q_rot, k_rot, preferred_element_type=jnp.float32) * (head_dim ** -0.5)
    causal = jnp.arange(seq_len)[:, None] >= jnp.arange(seq_len)[None, :]
    attn_probs = jax.nn.softmax(jnp.where(causal, scores, -1e30), axis=-1).astype(jnp.bfloat16)
    return jnp.einsum("bhqk,bhke->bhqe", attn_probs, values, preferred_element_type=jnp.float32).astype(jnp.bfloat16)


def branch_partials(normed, cosine, sine, w_q, b_q, w_k, b_k, w_v, b_v, w_o, w_up, b_up, w_down):
    def project(weight, bias):
        return jnp.einsum("bld,dhe->bhle", normed, weight, preferred_element_type=jnp.float32) + bias.astype(jnp.float32)[None, :, None, :]

    q_rot = apply_rotary(project(w_q, b_q), cosine, sine).astype(jnp.bfloat16)
    k_rot = apply_rotary(project(w_k, b_k), cosine, sine).astype(jnp.bfloat16)
    values = project(w_v, b_v).astype(jnp.bfloat16)
    attended = causal_attention(q_rot, k_rot, values)
    up_act = jax.nn.gelu(jnp.einsum("bld,df->blf", normed, w_up, preferred_element_type=jnp.float32) + b_up.astype(jnp.float32), approximate=True).astype(jnp.bfloat16)
    return (jnp.einsum("bhle,hed->bld", attended, w_o, preferred_element_type=jnp.float32)
            + jnp.einsum("blf,fd->bld", up_act, w_down, preferred_element_type=jnp.float32))


def solution(mesh):
    tp_size = mesh.shape["tp"]
    head_spec = P(None, None, "tp", None)
    head_bias_spec = P(None, "tp", None)
    in_specs = (P("dp", "tp", None), P(), P(), head_spec, head_bias_spec, head_spec, head_bias_spec, head_spec, head_bias_spec,
                P(None, "tp", None, None), P(), P(None, None, "tp"), P(None, "tp"), P(None, "tp", None), P())

    def local_program(x_loc, ln_gain, ln_bias, w_q, b_q, w_k, b_k, w_v, b_v, w_o, b_o, w_up, b_up, w_down, b_down):
        cosine, sine = rotary_tables(x_loc.shape[1] * tp_size)
        hidden = x_loc
        for layer in range(w_q.shape[0]):
            normed = layer_norm(hidden, ln_gain[layer], ln_bias[layer])
            gathered = lax.all_gather(normed, "tp", axis=1, tiled=True)
            part_sum = branch_partials(gathered, cosine, sine, w_q[layer], b_q[layer], w_k[layer], b_k[layer], w_v[layer], b_v[layer],
                                       w_o[layer], w_up[layer], b_up[layer], w_down[layer]).astype(jnp.bfloat16)
            returned = lax.psum_scatter(part_sum, "tp", scatter_dimension=1, tiled=True)
            hidden = (hidden.astype(jnp.float32) + returned.astype(jnp.float32) + b_o[layer].astype(jnp.float32)
                      + b_down[layer].astype(jnp.float32)).astype(jnp.bfloat16)
        return hidden

    return jax.shard_map(local_program, mesh=mesh, in_specs=in_specs, out_specs=P("dp", "tp", None), check_vma=False)
```

profile of v0, /device:TPU:21, one launch (start us, length us, event | category | flops | bytes accessed | tf_op | source)
XLA Modules:
  0.0 260.3 jit_solution(5029182267586353686)
XLA Ops:
  6.6 1.0 convert_reduce_fusion.1
  7.6 1.1 fusion.219
  8.7 0.8 slice_convert_fusion.7
  9.6 0.8 slice_convert_fusion.6
  10.4 1.7 fusion.222
  12.2 0.8 slice_convert_fusion.16
  14.5 0.8 slice_convert_fusion.12
  15.3 38.3 %all-gather.3.cloned.1.call-done = bf16[1,256,4096]{2,1,0:T(8,128)(2,1)} async-done(((bf16[1,16,4096]{2,1,0:T(8,128)(2,1)}), bf16[1,256,4096]{2,1,0:T(8,128)(2,1)}) %all-gather.3.cloned.1.call-update) | async-done | bytes 2097168 | tf_op jit(solution)/shard_map/all_gather | solution.py:67
  53.6 3.3 %fusion.123 = f32[1,1,256,256]{2,3,1,0:T(8,128)S(1)} fusion(bf16[2,4096,1,256]{3,1,2,0:T(8,128)(2,1)} %param.20, bf16[1,256,4096]{2,1,0:T(8,128)(2,1)} %all-gather.3.cloned.1.call-done, f32[256]{0:T(256)S(1)} %bitcast.309), kind=kOutput, calls=%fused_computation.69 | convolution fusion | flops 536936448 | bytes 4457472 | tf_op jit(solution)/shard_map/bld,dhe->bhle/dot_general | solution.py:44
  57.0 2.7 %fusion.128 = f32[1,256,1,256]{3,1,2,0:T(8,128)S(1)} fusion(bf16[2,4096,1,256]{3,1,2,0:T(8,128)(2,1)S(1)} %copy-done.3, bf16[1,256,4096]{2,1,0:T(8,128)(2,1)} %all-gather.3.cloned.1.call-done, f32[256]{0:T(256)S(1)} %bitcast.308), kind=kOutput, calls=%fused_computation.70 | convolution fusion | flops 536936448 | bytes 4457472 | tf_op jit(solution)/shard_map/bld,dhe->bhle/dot_general | solution.py:44
  60.2 2.5 convolution_convert_fusion.1
  62.8 12.5 %fusion.4 = f32[256,4096]{1,0:T(8,128)} fusion(bf16[2,1024,4096]{2,1,0:T(8,128)(2,1)} %param.28, bf16[2,4096,1024]{2,1,0:T(8,128)(2,1)} %param.26, bf16[1,256,4096]{2,1,0:T(8,128)(2,1)S(1)} %copy-done.5, f32[1024]{0:T(1024)S(1)} %bitcast.303), kind=kOutput, calls=%fused_computation.4 | convolution fusion | flops 4297588736 | bytes 23072768 | tf_op jit(solution)/shard_map/blf,fd->bld/dot_general | solution.py:52
  75.3 4.9 %fusion.15 = bf16[1,256,4096]{2,1,0:T(8,128)(2,1)} fusion(f32[256,4096]{1,0:T(8,128)} %fusion.4, bf16[256,256]{1,0:T(8,128)(2,1)S(1)} %convolution_convert_fusion.1, bf16[2,1,256,4096]{3,2,1,0:T(8,128)(2,1)} %param.24), kind=kOutput, calls=%fused_computation.17 | convolution fusion | flops 538968064 | bytes 8519680 | tf_op jit(solution)/shard_map/bhle,hed->bld/dot_general | solution.py:51
  80.5 52.1 %reduce-scatter.3.cloned.1.call-done = bf16[1,16,4096]{2,1,0:T(8,128)(2,1)} async-done(((bf16[1,256,4096]{2,1,0:T(8,128)(2,1)}), bf16[1,16,4096]{2,1,0:T(8,128)(2,1)}) %reduce-scatter.3.cloned.1.call-update) | async-done | bytes 131088 | tf_op jit(solution)/shard_map/reduce_scatter | solution.py:70
  132.6 1.1 convert_reduce_fusion
  133.9 0.8 fusion.218
  135.0 38.0 %all-gather.5.cloned.1.call-done = bf16[1,256,4096]{2,1,0:T(8,128)(2,1)} async-done(((bf16[1,16,4096]{2,1,0:T(8,128)(2,1)}), bf16[1,256,4096]{2,1,0:T(8,128)(2,1)}) %all-gather.5.cloned.1.call-update) | async-done | bytes 2097168 | tf_op jit(solution)/shard_map/all_gather | solution.py:67
  173.1 3.3 %fusion.98 = f32[1,1,256,256]{2,3,1,0:T(8,128)S(1)} fusion(bf16[2,4096,1,256]{3,1,2,0:T(8,128)(2,1)} %param.20, bf16[1,256,4096]{2,1,0:T(8,128)(2,1)} %all-gather.5.cloned.1.call-done, f32[256]{0:T(256)S(1)} %bitcast.306), kind=kOutput, calls=%fused_computation.64 | convolution fusion | flops 536936448 | bytes 4457472 | tf_op jit(solution)/shard_map/bld,dhe->bhle/dot_general | solution.py:44
  176.5 2.7 %fusion.108 = f32[1,1,256,256]{2,3,1,0:T(8,128)S(1)} fusion(bf16[2,4096,1,256]{3,1,2,0:T(8,128)(2,1)S(1)} %copy-done.4, bf16[1,256,4096]{2,1,0:T(8,128)(2,1)} %all-gather.5.cloned.1.call-done, f32[256]{0:T(256)S(1)} %bitcast.305), kind=kOutput, calls=%fused_computation.66 | convolution fusion | flops 536936448 | bytes 4457472 | tf_op jit(solution)/shard_map/bld,dhe->bhle/dot_general | solution.py:44
  179.8 12.5 %fusion = f32[256,4096]{1,0:T(8,128)} fusion(bf16[2,1024,4096]{2,1,0:T(8,128)(2,1)} %param.28, bf16[2,4096,1024]{2,1,0:T(8,128)(2,1)} %param.26, bf16[1,256,4096]{2,1,0:T(8,128)(2,1)S(1)} %copy-done.6, f32[1024]{0:T(1024)S(1)} %bitcast.302), kind=kOutput, calls=%fused_computation | convolution fusion | flops 4297588736 | bytes 23072768 | tf_op jit(solution)/shard_map/blf,fd->bld/dot_general | solution.py:52
  192.3 2.5 convolution_convert_fusion
  194.8 4.9 %fusion.14 = bf16[1,256,4096]{2,1,0:T(8,128)(2,1)} fusion(f32[256,4096]{1,0:T(8,128)} %fusion, bf16[256,256]{1,0:T(8,128)(2,1)S(1)} %convolution_convert_fusion, bf16[2,1,256,4096]{3,2,1,0:T(8,128)(2,1)} %param.24), kind=kOutput, calls=%fused_computation.16 | convolution fusion | flops 538968064 | bytes 8519680 | tf_op jit(solution)/shard_map/bhle,hed->bld/dot_general | solution.py:51
  199.8 52.3 %reduce-scatter.5.cloned.1.call-done = bf16[1,16,4096]{2,1,0:T(8,128)(2,1)} async-done(((bf16[1,256,4096]{2,1,0:T(8,128)(2,1)}), bf16[1,16,4096]{2,1,0:T(8,128)(2,1)}) %reduce-scatter.5.cloned.1.call-update) | async-done | bytes 131088 | tf_op jit(solution)/shard_map/reduce_scatter | solution.py:70
  252.1 1.6 fusion.228
  (41 shorter events, 3.6 us)
Async XLA Ops:
  6.5 47.0 %all-gather.3.cloned.1.call-start = ((), (), s32[]{:S(2)}) async-start(), calls=%async_computation.2 | async-start | bytes 2228224 | tf_op jit(solution)/shard_map/all_gather | solution.py:67
  12.1 120.5 %reduce-scatter.3.cloned.1.call-start = ((), (), s32[]{:S(2)}) async-start(), calls=%async_computation.3 | async-start | bytes 2228224 | tf_op jit(solution)/shard_map/reduce_scatter | solution.py:70
  53.5 3.4 %copy-start.3 = (bf16[2,4096,1,256]{3,1,2,0:T(8,128)(2,1)S(1)}, bf16[2,4096,1,256]{3,1,2,0:T(8,128)(2,1)}, u32[]{:S(2)}) copy-start(bf16[2,4096,1,256]{3,1,2,0:T(8,128)(2,1)} %param.18) | copy-start | bytes 12582916
  56.9 3.4 %copy-start.5 = (bf16[1,256,4096]{2,1,0:T(8,128)(2,1)S(1)}, bf16[1,256,4096]{2,1,0:T(8,128)(2,1)}, u32[]{:S(2)}) copy-start(bf16[1,256,4096]{2,1,0:T(8,128)(2,1)} %all-gather.3.cloned.1.call-done) | copy-start | bytes 6291460
  75.3 5.1 %copy-start.1 = (bf16[2,4096]{1,0:T(2,128)(2,1)S(1)}, bf16[2,4096]{1,0:T(2,128)(2,1)}, u32[]{:S(2)}) copy-start(bf16[2,4096]{1,0:T(2,128)(2,1)} %param.25) | copy-start | bytes 49156
  75.3 5.1 %copy-start.2 = (bf16[2,4096]{1,0:T(2,128)(2,1)S(1)}, bf16[2,4096]{1,0:T(2,128)(2,1)}, u32[]{:S(2)}) copy-start(bf16[2,4096]{1,0:T(2,128)(2,1)} %param.29) | copy-start | bytes 49156
  75.3 57.3 %copy-start = (bf16[1,16,4096]{2,1,0:T(8,128)(2,1)S(1)}, bf16[1,16,4096]{2,1,0:T(8,128)(2,1)}, u32[]{:S(2)}) copy-start(bf16[1,16,4096]{2,1,0:T(8,128)(2,1)} %param.15) | copy-start | bytes 393220
  80.3 92.8 %all-gather.5.cloned.1.call-start = ((), (), s32[]{:S(2)}) async-start(), calls=%async_computation.4 | async-start | bytes 2228224 | tf_op jit(solution)/shard_map/all_gather | solution.py:67
  134.8 117.3 %reduce-scatter.5.cloned.1.call-start = ((), (), s32[]{:S(2)}) async-start(), calls=%async_computation.5 | async-start | bytes 2228224 | tf_op jit(solution)/shard_map/reduce_scatter | solution.py:70
  173.1 3.4 %copy-start.4 = (bf16[2,4096,1,256]{3,1,2,0:T(8,128)(2,1)S(1)}, bf16[2,4096,1,256]{3,1,2,0:T(8,128)(2,1)}, u32[]{:S(2)}) copy-start(bf16[2,4096,1,256]{3,1,2,0:T(8,128)(2,1)} %param.18) | copy-start | bytes 12582916
  176.4 3.4 %copy-start.6 = (bf16[1,256,4096]{2,1,0:T(8,128)(2,1)S(1)}, bf16[1,256,4096]{2,1,0:T(8,128)(2,1)}, u32[]{:S(2)}) copy-start(bf16[1,256,4096]{2,1,0:T(8,128)(2,1)} %all-gather.5.cloned.1.call-done) | copy-start | bytes 6291460
Sparse Core Ops, SparseCore 0:
  12.3 41.2 all-gather.2
  80.4 52.1 reduce-scatter.2
  134.9 38.1 all-gather.4
  199.9 52.1 reduce-scatter.4
where the time goes:
time: 263 us; the launch traced here: 260 us
  waiting for transfers between devices  181 us (69%)
  matrix products  52.6 us (20%)
  between operations  13.3 us (5%)
  other arithmetic  12.8 us (5%)
    reduce_scatter x2, waiting for transfers between devices, local_program(): returned = lax.psum_scatter(part_sum, 'tp', scatter_dimension=1, tiled=True)  104 us
    all_gather x2, waiting for transfers between devices, local_program(): gathered = lax.all_gather(normed, 'tp', axis=1, tiled=True)  76.3 us
    dot_general x2, matrix products, branch_partials(): jnp.einsum('blf,fd->bld', up_act, w_down, preferred_element_type=jnp.floa...  25.1 us
    dot_general x4, matrix products, project(): jnp.einsum('bld,dhe->bhle', normed, weight, preferred_element_type=jnp.fl...  12.1 us
    dot_general x2, matrix products, branch_partials(): jnp.einsum('bhle,hed->bld', attended, w_o, preferred_element_type=jnp.flo...  9.82 us
  transfers between devices with their start and end apart: 4, of which 4 were waited for; matrix products, arithmetic and copies ran while one was open for 1% of the time, Pallas kernels for 0%

commit v1 on v0

v1 whole, which is shorter than its diff:
```python
import functools

import jax
import jax.numpy as jnp
import numpy as np
from jax import lax
from jax.experimental import pallas as pl
from jax.experimental.pallas import tpu as pltpu
from jax.sharding import PartitionSpec as P

ROT_DIM = 32
ROPE_BASE = 10000.0
LN_EPS = 1e-5
MESH = pl.DeviceIdType.MESH
F32 = jnp.float32
BF16 = jnp.bfloat16
CW, CCW = 0, 1


def row_positions(n_chips, rows):
    half, core, chip, row = np.meshgrid(np.arange(2), np.arange(2), np.arange(n_chips), np.arange(rows), indexing="ij")
    return (2 * rows * (2 * chip + core) + rows * half + row).reshape(-1)


def rotary_constants(positions):
    half = ROT_DIM // 2
    inv_freq = (1.0 / (np.float32(ROPE_BASE) ** (np.arange(half, dtype=np.float32) * np.float32(2.0 / ROT_DIM)))).astype(np.float32)
    angles = positions.astype(np.float32)[:, None] * inv_freq[None, :]
    cosine, sine = np.cos(angles), np.sin(angles)
    table = np.zeros((3, positions.size, 128), np.float32)
    table[0] = 1.0
    table[0, :, :half] = cosine
    table[0, :, half:ROT_DIM] = cosine
    table[1, :, :half] = -sine
    table[2, :, half:ROT_DIM] = sine
    return table


def kernel(cfg, x_hbm, gain_ref, lbias_ref, wq, wk, wv, wo, wup, wdown, bq_ref, bk_ref, bv_ref, bup_ref, bo_ref, bdown_ref,
           rot_hbm, mask_hbm, out_hbm,
           xv, gat, par, dbuf, slot, win, wout, qkv, act, rot, mask, outv,
           w_sem, io_sem, ag_s, ag_r, agd_s, agd_r, rsd_s, rsd_r, rs_s, rs_r):
    n_layers, n_chips, rows, width, head, ff = cfg
    half_w = width // 2
    m_rows = 2 * n_chips * rows
    me = lax.axis_index("tp")
    core = lax.rem(me, 2)
    chip = me // 2
    partner = chip * 2 + (1 - core)
    last = n_chips // 2

    def at_chip(offset):
        return lax.rem(chip + offset + 2 * n_chips, n_chips)

    next_dev = (at_chip(1) * 2 + core, at_chip(-1) * 2 + core)

    def cols(ch):
        return pl.ds(ch * half_w, half_w)

    x_copy = pltpu.make_async_copy(x_hbm.at[0], xv, io_sem.at[0])
    x_copy.start()
    rot_copy = pltpu.make_async_copy(rot_hbm, rot, io_sem.at[1])
    mask_copy = pltpu.make_async_copy(mask_hbm, mask, io_sem.at[2])

    def weight_copies(layer):
        copies = []
        for i, src in enumerate((wq, wk, wv)):
            copies.append(pltpu.make_async_copy(src.at[layer], win.at[layer, :, pl.ds(i * head, head)], w_sem.at[layer, i]))
        copies.append(pltpu.make_async_copy(wup.at[layer], win.at[layer, :, pl.ds(3 * head, ff)], w_sem.at[layer, 3]))
        copies.append(pltpu.make_async_copy(wo.at[layer], wout.at[layer, pl.ds(0, head), :], w_sem.at[layer, 4]))
        copies.append(pltpu.make_async_copy(wdown.at[layer], wout.at[layer, pl.ds(head, ff), :], w_sem.at[layer, 5]))
        return copies

    weights = [weight_copies(layer) for layer in range(n_layers)]
    barrier = pltpu.get_barrier_semaphore()
    for dev in (next_dev[CW], next_dev[CCW], partner):
        pl.semaphore_signal(barrier, inc=1, device_id={"tp": dev}, device_id_type=MESH)
    rot_copy.start()
    mask_copy.start()
    for layer in range(n_layers):
        for copy in weights[layer]:
            copy.start()

    def ag_copy(layer, x, d, s, ch):
        src = at_chip(-s if d == CW else s)
        ref = gat.at[layer, x, core, src, :, cols(ch)]
        return pltpu.make_async_remote_copy(ref, ref, ag_s.at[layer, x, d, s, ch], ag_r.at[layer, x, d, s, ch],
                                            device_id={"tp": next_dev[d]}, device_id_type=MESH)

    def agd_copy(layer, x, i, offset):
        ref = gat.at[layer, x, core, at_chip(offset)]
        return pltpu.make_async_remote_copy(ref, ref, agd_s.at[layer, x, i], agd_r.at[layer, x, i],
                                            device_id={"tp": partner}, device_id_type=MESH)

    def ag_incoming(layer, x, d, s, ch):
        src = at_chip(-(s + 1) if d == CW else s + 1)
        ref = gat.at[layer, x, core, src, :, cols(ch)]
        return pltpu.make_async_remote_copy(ref, ref, ag_s.at[layer, x, d, s, ch], ag_r.at[layer, x, d, s, ch],
                                            device_id={"tp": next_dev[d]}, device_id_type=MESH)

    agd_offsets = [0] + [o for s in range(1, last) for o in (-s, s)] + [last]
    pending = []

    def go(copy):
        copy.start()
        pending.append(copy)

    def has_hop(d, s, ch):
        return s < last - 1 or ch == d

    def layer_norm(layer, x):
        value = xv[pl.ds(x * rows, rows), :].astype(F32)
        mean = jnp.mean(value, axis=-1, keepdims=True)
        centered = value - mean
        variance = jnp.mean(centered * centered, axis=-1, keepdims=True)
        normed = centered * lax.rsqrt(variance + LN_EPS) * gain_ref[pl.ds(layer, 1), :].astype(F32) + lbias_ref[pl.ds(layer, 1), :].astype(F32)
        gat[layer, x, core, chip] = normed.astype(BF16)

    def ag_start(layer, x):
        for ch in range(2):
            for d in (CW, CCW):
                go(ag_copy(layer, x, d, 0, ch))
        go(agd_copy(layer, x, 0, 0))

    def ag_hop(layer, x, s):
        for ch in range(2):
            for d in (CW, CCW):
                ag_incoming(layer, x, d, s - 1, ch).wait_recv()
                if has_hop(d, s, ch):
                    go(ag_copy(layer, x, d, s, ch))
        for j, o in enumerate((-s, s)):
            go(agd_copy(layer, x, 2 * s - 1 + j, o))

    def ag_last(layer, x):
        for d in (CW, CCW):
            ag_incoming(layer, x, d, last - 1, d).wait_recv()
        go(agd_copy(layer, x, len(agd_offsets) - 1, last))

    def ag_dwait(layer, x):
        for i, o in enumerate(agd_offsets):
            ref = gat.at[layer, x, 1 - core, at_chip(o)]
            pltpu.make_async_remote_copy(ref, ref, agd_s.at[layer, x, i], agd_r.at[layer, x, i],
                                         device_id={"tp": partner}, device_id_type=MESH).wait_recv()

    def normed_rows(layer, x):
        return gat[layer, x].reshape(m_rows, width)

    def project_qkv(layer, x):
        rows_x = pl.ds(x * m_rows, m_rows)
        out = jnp.dot(normed_rows(layer, x), win[layer, :, pl.ds(0, 3 * head)], preferred_element_type=F32)
        for i, bias in enumerate((bq_ref, bk_ref, bv_ref)):
            value = out[:, i * head:(i + 1) * head] + bias[pl.ds(layer, 1), :].astype(F32)
            if i < 2:
                low = value[:, :128]
                low = (low * rot[0, rows_x, :] + pltpu.roll(low, 128 - ROT_DIM // 2, 1) * rot[1, rows_x, :]
                       + pltpu.roll(low, ROT_DIM // 2, 1) * rot[2, rows_x, :])
                qkv[i, rows_x, pl.ds(0, 128)] = low.astype(BF16)
                qkv[i, rows_x, pl.ds(128, head - 128)] = value[:, 128:].astype(BF16)
            else:
                qkv[i, rows_x, :] = value.astype(BF16)

    def project_up(layer, x, tile, width_n):
        col = pl.ds(tile * width_n, width_n)
        out = jnp.dot(normed_rows(layer, x), win[layer, :, pl.ds(3 * head + tile * width_n, width_n)], preferred_element_type=F32)
        out = out + bup_ref[pl.ds(layer, 1), col].astype(F32)
        act[x, :, pl.ds(head + tile * width_n, width_n)] = jax.nn.gelu(out, approximate=True).astype(BF16)

    def attend():
        scores = lax.dot_general(qkv[0], qkv[1], (((1,), (1,)), ((), ())), preferred_element_type=F32) * (head ** -0.5)
        scores = jnp.where(mask[...] > 0, scores, -1e30)
        top = jnp.max(scores, axis=-1, keepdims=True)
        e = jnp.exp(scores - top)
        probs = (e / jnp.sum(e, axis=-1, keepdims=True)).astype(BF16)
        out = jnp.dot(probs, qkv[2], preferred_element_type=F32).astype(BF16)
        for x in range(2):
            act[x, :, pl.ds(0, head)] = out[x * m_rows:(x + 1) * m_rows]

    def rsd_copy(layer, x, ch):
        return pltpu.make_async_remote_copy(par.at[x, 1 - core, :, :, cols(ch)], dbuf.at[layer, x, :, :, cols(ch)],
                                            rsd_s.at[layer, x, ch], rsd_r.at[layer, x, ch],
                                            device_id={"tp": partner}, device_id_type=MESH)

    def rs_part(layer, x, ch):
        tile = 512 if half_w % 512 == 0 else half_w

        def body(i, carry):
            start = pl.multiple_of(ch * half_w + i * tile, tile)
            out = jnp.dot(act[x], wout[layer, :, pl.ds(start, tile)], preferred_element_type=F32)
            par[x, :, :, :, pl.ds(start, tile)] = out.astype(BF16).reshape(2, n_chips, rows, tile)
            return carry

        lax.fori_loop(0, half_w // tile, body, 0)
        go(rsd_copy(layer, x, ch))

    def rs_copy(layer, x, d, t, ch):
        dest = at_chip(last - t if d == CW else t - last)
        return pltpu.make_async_remote_copy(par.at[x, core, dest, :, cols(ch)], slot.at[layer, x, d, t, :, cols(ch)],
                                            rs_s.at[layer, x, d, t, ch], rs_r.at[layer, x, d, t, ch],
                                            device_id={"tp": next_dev[d]}, device_id_type=MESH)

    def rs_first(d, ch):
        return 0 if ch == d else 1

    def rs_hop(layer, x, d, t, ch):
        dest = at_chip(last - t if d == CW else t - last)
        total = par[x, core, dest, :, cols(ch)].astype(F32) + dbuf[layer, x, dest, :, cols(ch)].astype(F32)
        if t > rs_first(d, ch):
            rs_copy(layer, x, d, t - 1, ch).wait_recv()
            total = total + slot[layer, x, d, t - 1, :, cols(ch)].astype(F32)
        par[x, core, dest, :, cols(ch)] = total.astype(BF16)
        go(rs_copy(layer, x, d, t, ch))

    def rs_begin(layer, x, ch):
        rsd_copy(layer, x, ch).wait_recv()
        for d in (CW, CCW):
            rs_hop(layer, x, d, rs_first(d, ch), ch)

    def rs_step(layer, x, t):
        for ch in range(2):
            for d in (CW, CCW):
                if t > rs_first(d, ch):
                    rs_hop(layer, x, d, t, ch)

    def rs_final(layer, x):
        for ch in range(2):
            total = par[x, core, chip, :, cols(ch)].astype(F32) + dbuf[layer, x, chip, :, cols(ch)].astype(F32)
            for d in (CW, CCW):
                rs_copy(layer, x, d, last - 1, ch).wait_recv()
                total = total + slot[layer, x, d, last - 1, :, cols(ch)].astype(F32)
            total = (total + bo_ref[pl.ds(layer, 1), cols(ch)].astype(F32) + bdown_ref[pl.ds(layer, 1), cols(ch)].astype(F32)
                     + xv[pl.ds(x * rows, rows), cols(ch)].astype(F32))
            target = xv if layer < n_layers - 1 else outv
            target[pl.ds(x * rows, rows), cols(ch)] = total.astype(BF16)

    def drain():
        for copy in pending:
            copy.wait_send()
        pending.clear()

    x_copy.wait()
    for x in range(2):
        layer_norm(0, x)
    pl.semaphore_wait(barrier, 3)
    for x in range(2):
        ag_start(0, x)
    rot_copy.wait()
    mask_copy.wait()
    up_tile = 512 if ff % 512 == 0 else ff
    n_up = ff // up_tile
    for layer in range(n_layers):
        for s in range(1, last):
            for x in range(2):
                ag_hop(layer, x, s)
        ag_last(layer, 0)
        for i in range(3):
            weights[layer][i].wait()
        ag_dwait(layer, 0)
        project_qkv(layer, 0)
        ag_last(layer, 1)
        weights[layer][3].wait()
        for tile in range(n_up):
            project_up(layer, 0, tile, up_tile)
        ag_dwait(layer, 1)
        project_qkv(layer, 1)
        attend()
        for i in (4, 5):
            weights[layer][i].wait()
        rs_part(layer, 0, 0)
        rs_part(layer, 0, 1)
        rs_begin(layer, 0, 0)
        project_up(layer, 1, 0, up_tile)
        rs_begin(layer, 0, 1)
        for tile in range(1, n_up):
            project_up(layer, 1, tile, up_tile)
        rs_step(layer, 0, 1)
        rs_part(layer, 1, 0)
        rs_part(layer, 1, 1)
        rs_step(layer, 0, 2)
        rs_begin(layer, 1, 0)
        rs_begin(layer, 1, 1)
        rs_step(layer, 0, 3)
        for t in range(1, last):
            rs_step(layer, 1, t)
        for x in range(2):
            rs_final(layer, x)
            if layer < n_layers - 1:
                layer_norm(layer + 1, x)
        drain()
        if layer < n_layers - 1:
            for x in range(2):
                ag_start(layer + 1, x)
    out_copy = pltpu.make_async_copy(outv, out_hbm.at[0], io_sem.at[3])
    out_copy.start()
    out_copy.wait()


def solution(mesh):
    tp = mesh.shape["tp"]
    n_chips = tp // 2
    head_spec = P(None, None, "tp", None)
    head_bias_spec = P(None, "tp", None)
    in_specs = (P("dp", "tp", None), P(), P(), head_spec, head_bias_spec, head_spec, head_bias_spec, head_spec, head_bias_spec,
                P(None, "tp", None, None), P(), P(None, None, "tp"), P(None, "tp"), P(None, "tp", None), P())

    def local_program(x_loc, ln_gain, ln_bias, w_q, b_q, w_k, b_k, w_v, b_v, w_o, b_o, w_up, b_up, w_down, b_down):
        n_layers, width, _, head = w_q.shape
        ff = w_up.shape[2]
        rows = x_loc.shape[1] // 2
        m_rows = 2 * n_chips * rows
        positions = row_positions(n_chips, rows)
        rot = jnp.asarray(rotary_constants(positions))
        mask = jnp.asarray((positions[:, None] >= positions[None, :]).astype(np.float32))
        flat = lambda w: w.reshape(n_layers, width, head)
        bias = lambda b: b.reshape(n_layers, head)
        cfg = (n_layers, n_chips, rows, width, head, ff)
        any_spec = pl.BlockSpec(memory_space=pl.ANY)
        vmem_spec = pl.BlockSpec(memory_space=pltpu.VMEM)
        dma = pltpu.SemaphoreType.DMA
        hops = n_chips // 2
        return pl.pallas_call(
            functools.partial(kernel, cfg),
            out_shape=jax.ShapeDtypeStruct(x_loc.shape, x_loc.dtype),
            in_specs=[any_spec, vmem_spec, vmem_spec] + [any_spec] * 6 + [vmem_spec] * 6 + [any_spec] * 2,
            out_specs=any_spec,
            scratch_shapes=[
                pltpu.VMEM((2 * rows, width), BF16),
                pltpu.VMEM((n_layers, 2, 2, n_chips, rows, width), BF16),
                pltpu.VMEM((2, 2, n_chips, rows, width), BF16),
                pltpu.VMEM((n_layers, 2, n_chips, rows, width), BF16),
                pltpu.VMEM((n_layers, 2, 2, hops, rows, width), BF16),
                pltpu.VMEM((n_layers, width, 3 * head + ff), BF16),
                pltpu.VMEM((n_layers, head + ff, width), BF16),
                pltpu.VMEM((3, 2 * m_rows, head), BF16),
                pltpu.VMEM((2, m_rows, head + ff), BF16),
                pltpu.VMEM((3, 2 * m_rows, 128), F32),
                pltpu.VMEM((2 * m_rows, 2 * m_rows), F32),
                pltpu.VMEM((2 * rows, width), BF16),
                dma((n_layers, 6)),
                dma((4,)),
                dma((n_layers, 2, 2, hops, 2)),
                dma((n_layers, 2, 2, hops, 2)),
                dma((n_layers, 2, n_chips)),
                dma((n_layers, 2, n_chips)),
                dma((n_layers, 2, 2)),
                dma((n_layers, 2, 2)),
                dma((n_layers, 2, 2, hops, 2)),
                dma((n_layers, 2, 2, hops, 2)),
            ],
            compiler_params=pltpu.CompilerParams(collective_id=0, has_side_effects=True, vmem_limit_bytes=67_000_000),
            name="decoder",
        )(x_loc, ln_gain, ln_bias, flat(w_q), flat(w_k), flat(w_v), w_o.reshape(n_layers, head, width), w_up, w_down,
          bias(b_q), bias(b_k), bias(b_v), b_up, b_o, b_down, rot, mask)

    return jax.shard_map(local_program, mesh=mesh, in_specs=in_specs, out_specs=P("dp", "tp", None), check_vma=False)
```

time: 263 us -> 114 us (0.43)
  the two profiles are of different devices: /device:TPU:21 before, /device:TPU:28 now
where the time goes in v1:
time: 114 us; the launch traced here: 113 us
  Pallas kernels  112 us (98%)
  local copies, waits for them, and re-layouts  1.57 us (1%)
    pallas_call x1, Pallas kernels, local_program(): pl.pallas_call(functools.partial(kernel, cfg), out_shape=jax.ShapeDtypeSt...  112 us

profile of v1, /device:TPU:28, one launch (start us, length us, event | category | flops | bytes accessed | tf_op | source)
XLA Modules:
  0.0 113.4 jit_solution(9085140188078215937)
XLA Ops:
  0.0 111.8 %decoder.1 = bf16[1,16,4096]{2,1,0:T(8,128)(2,1)} custom-call(bf16[1,16,4096]{2,1,0:T(8,128)(2,1)} %x_hbm.1, bf16[2,4096]{1,0:T(2,128)(2,1)} %gain_ref.1, bf16[2,4096]{1,0:T(2,128)(2,1)} %lbias_ref.1, bf16[2,4096,256]{2,1,0:T(8,128)(2,1)} %bitcast.7, bf16[2,4096,256]{2,1,0:T(8,128)(2,1)} %bitcast.8, bf16[2,4096,256]{2,1,0:T(8,128)(2,1)} %bitcast.9, ...), custom_call_target="tpu_custom_call" | custom-call | tf_op jit(solution)/shard_map/decoder/pallas_call | solution.py:320
  111.8 1.6 %copy.19 = bf16[1,16,4096]{2,1,0:T(8,128)(2,1)} copy(bf16[1,16,4096]{2,1,0:T(8,128)(2,1)} %decoder.1) | data formatting | bytes 262144

commit v2 on v1

--- a/solution.py
+++ b/solution.py
@@ -15,6 +15,7 @@
 F32 = jnp.float32
 BF16 = jnp.bfloat16
 CW, CCW = 0, 1
+CHUNKS = 4
 
 
 def row_positions(n_chips, rows):
@@ -57,6 +58,14 @@
     def cols(ch):
         return pl.ds(ch * half_w, half_w)
 
+    chunk_w = width // CHUNKS
+
+    def chunk(q):
+        return pl.ds(q * chunk_w, chunk_w)
+
+    def owner(q):
+        return q * 2 // CHUNKS
+
     x_copy = pltpu.make_async_copy(x_hbm.at[0], xv, io_sem.at[0])
     x_copy.start()
     rot_copy = pltpu.make_async_copy(rot_hbm, rot, io_sem.at[1])
@@ -77,9 +86,8 @@
         pl.semaphore_signal(barrier, inc=1, device_id={"tp": dev}, device_id_type=MESH)
     rot_copy.start()
     mask_copy.start()
-    for layer in range(n_layers):
-        for copy in weights[layer]:
-            copy.start()
+    for copy in weights[0]:
+        copy.start()
 
     def ag_copy(layer, x, d, s, ch):
         src = at_chip(-s if d == CW else s)
@@ -99,11 +107,11 @@
                                             device_id={"tp": next_dev[d]}, device_id_type=MESH)
 
     agd_offsets = [0] + [o for s in range(1, last) for o in (-s, s)] + [last]
-    pending = []
-
-    def go(copy):
+    gather_sends, scatter_sends = [], []
+
+    def go(copy, sends):
         copy.start()
-        pending.append(copy)
+        sends.append(copy)
 
     def has_hop(d, s, ch):
         return s < last - 1 or ch == d
@@ -119,22 +127,22 @@
     def ag_start(layer, x):
         for ch in range(2):
             for d in (CW, CCW):
-                go(ag_copy(layer, x, d, 0, ch))
-        go(agd_copy(layer, x, 0, 0))
+                go(ag_copy(layer, x, d, 0, ch), gather_sends)
+        go(agd_copy(layer, x, 0, 0), gather_sends)
 
     def ag_hop(layer, x, s):
         for ch in range(2):
             for d in (CW, CCW):
                 ag_incoming(layer, x, d, s - 1, ch).wait_recv()
                 if has_hop(d, s, ch):
-                    go(ag_copy(layer, x, d, s, ch))
+                    go(ag_copy(layer, x, d, s, ch), gather_sends)
         for j, o in enumerate((-s, s)):
-            go(agd_copy(layer, x, 2 * s - 1 + j, o))
+            go(agd_copy(layer, x, 2 * s - 1 + j, o), gather_sends)
 
     def ag_last(layer, x):
         for d in (CW, CCW):
             ag_incoming(layer, x, d, last - 1, d).wait_recv()
-        go(agd_copy(layer, x, len(agd_offsets) - 1, last))
+        go(agd_copy(layer, x, len(agd_offsets) - 1, last), gather_sends)
 
     def ag_dwait(layer, x):
         for i, o in enumerate(agd_offsets):
@@ -175,123 +183,161 @@
         for x in range(2):
             act[x, :, pl.ds(0, head)] = out[x * m_rows:(x + 1) * m_rows]
 
-    def rsd_copy(layer, x, ch):
-        return pltpu.make_async_remote_copy(par.at[x, 1 - core, :, :, cols(ch)], dbuf.at[layer, x, :, :, cols(ch)],
-                                            rsd_s.at[layer, x, ch], rsd_r.at[layer, x, ch],
+    def rsd_copy(layer, x, q):
+        return pltpu.make_async_remote_copy(par.at[x, 1 - core, :, :, chunk(q)], dbuf.at[layer, x, :, :, chunk(q)],
+                                            rsd_s.at[layer, x, q], rsd_r.at[layer, x, q],
                                             device_id={"tp": partner}, device_id_type=MESH)
 
-    def rs_part(layer, x, ch):
-        tile = 512 if half_w % 512 == 0 else half_w
-
-        def body(i, carry):
-            start = pl.multiple_of(ch * half_w + i * tile, tile)
-            out = jnp.dot(act[x], wout[layer, :, pl.ds(start, tile)], preferred_element_type=F32)
-            par[x, :, :, :, pl.ds(start, tile)] = out.astype(BF16).reshape(2, n_chips, rows, tile)
-            return carry
-
-        lax.fori_loop(0, half_w // tile, body, 0)
-        go(rsd_copy(layer, x, ch))
-
-    def rs_copy(layer, x, d, t, ch):
+    def rs_part(layer, x, q):
+        out = jnp.dot(act[x], wout[layer, :, chunk(q)], preferred_element_type=F32)
+        par[x, :, :, :, chunk(q)] = out.astype(BF16).reshape(2, n_chips, rows, chunk_w)
+        go(rsd_copy(layer, x, q), scatter_sends)
+
+    def rs_copy(layer, x, d, t, q):
         dest = at_chip(last - t if d == CW else t - last)
-        return pltpu.make_async_remote_copy(par.at[x, core, dest, :, cols(ch)], slot.at[layer, x, d, t, :, cols(ch)],
-                                            rs_s.at[layer, x, d, t, ch], rs_r.at[layer, x, d, t, ch],
+        return pltpu.make_async_remote_copy(par.at[x, core, dest, :, chunk(q)], slot.at[layer, x, d, t, :, chunk(q)],
+                                            rs_s.at[layer, x, d, t, q], rs_r.at[layer, x, d, t, q],
                                             device_id={"tp": next_dev[d]}, device_id_type=MESH)
 
-    def rs_first(d, ch):
-        return 0 if ch == d else 1
-
-    def rs_hop(layer, x, d, t, ch):
+    def rs_first(d, q):
+        return 0 if owner(q) == d else 1
+
+    def rs_hop(layer, x, d, t, q):
         dest = at_chip(last - t if d == CW else t - last)
-        total = par[x, core, dest, :, cols(ch)].astype(F32) + dbuf[layer, x, dest, :, cols(ch)].astype(F32)
-        if t > rs_first(d, ch):
-            rs_copy(layer, x, d, t - 1, ch).wait_recv()
-            total = total + slot[layer, x, d, t - 1, :, cols(ch)].astype(F32)
-        par[x, core, dest, :, cols(ch)] = total.astype(BF16)
-        go(rs_copy(layer, x, d, t, ch))
-
-    def rs_begin(layer, x, ch):
-        rsd_copy(layer, x, ch).wait_recv()
+        total = par[x, core, dest, :, chunk(q)].astype(F32) + dbuf[layer, x, dest, :, chunk(q)].astype(F32)
+        if t > rs_first(d, q):
+            rs_copy(layer, x, d, t - 1, q).wait_recv()
+            total = total + slot[layer, x, d, t - 1, :, chunk(q)].astype(F32)
+        par[x, core, dest, :, chunk(q)] = total.astype(BF16)
+        go(rs_copy(layer, x, d, t, q), scatter_sends)
+
+    def rs_begin(layer, x, q):
+        rsd_copy(layer, x, q).wait_recv()
         for d in (CW, CCW):
-            rs_hop(layer, x, d, rs_first(d, ch), ch)
-
-    def rs_step(layer, x, t):
-        for ch in range(2):
+            rs_hop(layer, x, d, rs_first(d, q), q)
+
+    def rs_step(layer, x, t, q):
+        for d in (CW, CCW):
+            if t > rs_first(d, q):
+                rs_hop(layer, x, d, t, q)
+
+    def rs_final(layer, x):
+        for q in range(CHUNKS):
+            total = par[x, core, chip, :, chunk(q)].astype(F32) + dbuf[layer, x, chip, :, chunk(q)].astype(F32)
             for d in (CW, CCW):
-                if t > rs_first(d, ch):
-                    rs_hop(layer, x, d, t, ch)
-
-    def rs_final(layer, x):
-        for ch in range(2):
-            total = par[x, core, chip, :, cols(ch)].astype(F32) + dbuf[layer, x, chip, :, cols(ch)].astype(F32)
-            for d in (CW, CCW):
-                rs_copy(layer, x, d, last - 1, ch).wait_recv()
-                total = total + slot[layer, x, d, last - 1, :, cols(ch)].astype(F32)
-            total = (total + bo_ref[pl.ds(layer, 1), cols(ch)].astype(F32) + bdown_ref[pl.ds(layer, 1), cols(ch)].astype(F32)
-                     + xv[pl.ds(x * rows, rows), cols(ch)].astype(F32))
+                rs_copy(layer, x, d, last - 1, q).wait_recv()
+                total = total + slot[layer, x, d, last - 1, :, chunk(q)].astype(F32)
+            total = (total + bo_ref[pl.ds(layer, 1), chunk(q)].astype(F32) + bdown_ref[pl.ds(layer, 1), chunk(q)].astype(F32)
+                     + xv[pl.ds(x * rows, rows), chunk(q)].astype(F32))
             target = xv if layer < n_layers - 1 else outv
-            target[pl.ds(x * rows, rows), cols(ch)] = total.astype(BF16)
-
-    def drain():
-        for copy in pending:
+            target[pl.ds(x * rows, rows), chunk(q)] = total.astype(BF16)
+
+    def drain(sends):
+        for copy in sends:
             copy.wait_send()
-        pending.clear()
+        sends.clear()
+
+    def store(x):
+        rows_x = pl.ds(x * rows, rows)
+        return pltpu.make_async_copy(outv.at[rows_x], out_hbm.at[0, rows_x], io_sem.at[3 + x])
+
+    def weight_wait(layer, i):
+        weights[layer][i].wait()
+
+    def run(event, *place):
+        event(*place)
 
     x_copy.wait()
     for x in range(2):
-        layer_norm(0, x)
+        run(layer_norm, 0, x)
     pl.semaphore_wait(barrier, 3)
     for x in range(2):
-        ag_start(0, x)
-    rot_copy.wait()
-    mask_copy.wait()
-    up_tile = 512 if ff % 512 == 0 else ff
-    n_up = ff // up_tile
+        run(ag_start, 0, x)
     for layer in range(n_layers):
-        for s in range(1, last):
-            for x in range(2):
-                ag_hop(layer, x, s)
-        ag_last(layer, 0)
-        for i in range(3):
-            weights[layer][i].wait()
-        ag_dwait(layer, 0)
-        project_qkv(layer, 0)
-        ag_last(layer, 1)
-        weights[layer][3].wait()
-        for tile in range(n_up):
-            project_up(layer, 0, tile, up_tile)
-        ag_dwait(layer, 1)
-        project_qkv(layer, 1)
-        attend()
-        for i in (4, 5):
-            weights[layer][i].wait()
-        rs_part(layer, 0, 0)
-        rs_part(layer, 0, 1)
-        rs_begin(layer, 0, 0)
-        project_up(layer, 1, 0, up_tile)
-        rs_begin(layer, 0, 1)
-        for tile in range(1, n_up):
-            project_up(layer, 1, tile, up_tile)
-        rs_step(layer, 0, 1)
-        rs_part(layer, 1, 0)
-        rs_part(layer, 1, 1)
-        rs_step(layer, 0, 2)
-        rs_begin(layer, 1, 0)
-        rs_begin(layer, 1, 1)
-        rs_step(layer, 0, 3)
-        for t in range(1, last):
-            rs_step(layer, 1, t)
-        for x in range(2):
-            rs_final(layer, x)
-            if layer < n_layers - 1:
-                layer_norm(layer + 1, x)
-        drain()
-        if layer < n_layers - 1:
-            for x in range(2):
-                ag_start(layer + 1, x)
-    out_copy = pltpu.make_async_copy(outv, out_hbm.at[0], io_sem.at[3])
-    out_copy.start()
-    out_copy.wait()
+        final = layer == n_layers - 1
+
+        def upper(x, tile, tiles):
+            run(project_up, layer, x, tile, ff // tiles)
+
+        def each(event, x, *place):
+            for q in place[-1]:
+                run(event, layer, x, *place[:-1], q)
+
+        if layer == 0:
+            for s in range(1, last):
+                for x in range(2):
+                    run(ag_hop, layer, x, s)
+        else:
+            for s in range(2, last):
+                for x in range(2):
+                    run(ag_hop, layer, x, s)
+        run(ag_last, layer, 0)
+        if layer == 0:
+            rot_copy.wait()
+            mask_copy.wait()
+            for i in range(3):
+                run(weight_wait, layer, i)
+        run(ag_dwait, layer, 0)
+        run(project_qkv, layer, 0)
+        run(ag_last, layer, 1)
+        if layer == 0:
+            run(weight_wait, layer, 3)
+        upper(0, 0, 1)
+        run(ag_dwait, layer, 1)
+        run(project_qkv, layer, 1)
+        run(attend)
+        if not final:
+            for copy in weights[layer + 1]:
+                copy.start()
+        run(weight_wait, layer, 4)
+        run(weight_wait, layer, 5)
+        run(drain, scatter_sends)
+        each(rs_part, 0, (0, 1, 2))
+        each(rs_begin, 0, (0,))
+        each(rs_part, 0, (3,))
+        each(rs_begin, 0, (1,))
+        upper(1, 0, 2)
+        each(rs_begin, 0, (2, 3))
+        upper(1, 1, 2)
+        each(rs_part, 1, (0,))
+        each(rs_step, 0, 1, (0, 1))
+        each(rs_part, 1, (1,))
+        each(rs_step, 0, 1, (2, 3))
+        each(rs_part, 1, (2,))
+        each(rs_begin, 1, (0,))
+        each(rs_part, 1, (3,))
+        each(rs_begin, 1, (1,))
+        each(rs_step, 0, 2, (0, 1))
+        each(rs_begin, 1, (2,))
+        each(rs_step, 0, 2, (2, 3))
+        each(rs_begin, 1, (3,))
+        each(rs_step, 1, 1, (0, 1))
+        each(rs_step, 0, 3, (0, 1))
+        each(rs_step, 1, 1, (2, 3))
+        each(rs_step, 0, 3, (2, 3))
+        each(rs_step, 1, 2, (0, 1))
+        run(rs_final, layer, 0)
+        if not final:
+            run(layer_norm, layer + 1, 0)
+            run(ag_start, layer + 1, 0)
+        else:
+            store(0).start()
+        each(rs_step, 1, 2, (2, 3))
+        each(rs_step, 1, 3, (0, 1, 2, 3))
+        if not final:
+            run(ag_hop, layer + 1, 0, 1)
+        run(rs_final, layer, 1)
+        if not final:
+            run(layer_norm, layer + 1, 1)
+            run(ag_start, layer + 1, 1)
+            run(ag_hop, layer + 1, 1, 1)
+            for i in range(4):
+                run(weight_wait, layer + 1, i)
+    store(1).start()
+    run(drain, scatter_sends)
+    run(drain, gather_sends)
+    for x in range(2):
+        store(x).wait()
 
 
 def solution(mesh):
@@ -336,15 +382,15 @@
                 pltpu.VMEM((2 * m_rows, 2 * m_rows), F32),
                 pltpu.VMEM((2 * rows, width), BF16),
                 dma((n_layers, 6)),
-                dma((4,)),
+                dma((5,)),
                 dma((n_layers, 2, 2, hops, 2)),
                 dma((n_layers, 2, 2, hops, 2)),
                 dma((n_layers, 2, n_chips)),
                 dma((n_layers, 2, n_chips)),
-                dma((n_layers, 2, 2)),
-                dma((n_layers, 2, 2)),
-                dma((n_layers, 2, 2, hops, 2)),
-                dma((n_layers, 2, 2, hops, 2)),
+                dma((n_layers, 2, CHUNKS)),
+                dma((n_layers, 2, CHUNKS)),
+                dma((n_layers, 2, 2, hops, CHUNKS)),
+                dma((n_layers, 2, 2, hops, CHUNKS)),
             ],
             compiler_params=pltpu.CompilerParams(collective_id=0, has_side_effects=True, vmem_limit_bytes=67_000_000),
             name="decoder",

time: 114 us -> 99.6 us (0.87)
  the two profiles are of different devices: /device:TPU:28 before, /device:TPU:22 now
where the time goes in v2:
time: 99.6 us; the launch traced here: 99.4 us
  Pallas kernels  97.8 us (98%)
  local copies, waits for them, and re-layouts  1.57 us (2%)
    pallas_call x1, Pallas kernels, local_program(): pl.pallas_call(functools.partial(kernel, cfg), out_shape=jax.ShapeDtypeSt...  97.8 us

profile of v2, /device:TPU:22, one launch (start us, length us, event | category | flops | bytes accessed | tf_op | source)
XLA Modules:
  0.0 99.4 jit_solution(3039303791575468249)
XLA Ops:
  0.0 97.8 %decoder.1 = bf16[1,16,4096]{2,1,0:T(8,128)(2,1)} custom-call(bf16[1,16,4096]{2,1,0:T(8,128)(2,1)} %x_hbm.1, bf16[2,4096]{1,0:T(2,128)(2,1)} %gain_ref.1, bf16[2,4096]{1,0:T(2,128)(2,1)} %lbias_ref.1, bf16[2,4096,256]{2,1,0:T(8,128)(2,1)} %bitcast.7, bf16[2,4096,256]{2,1,0:T(8,128)(2,1)} %bitcast.8, bf16[2,4096,256]{2,1,0:T(8,128)(2,1)} %bitcast.9, ...), custom_call_target="tpu_custom_call" | custom-call | tf_op jit(solution)/shard_map/decoder/pallas_call | solution.py:366
  97.8 1.6 %copy.19 = bf16[1,16,4096]{2,1,0:T(8,128)(2,1)} copy(bf16[1,16,4096]{2,1,0:T(8,128)(2,1)} %decoder.1) | data formatting | bytes 262144
